TPU v7x, 32 devices: a whole 2x2x4 slice. The times are simulated.
32 devices in a mesh: dp: 2 (over core), layer: 2 (over x), col: 8 (over z, y).
Axes of the slice: x: 2, y: 2, z: 4, core: 2. Of those that a mesh axis runs over, the one named last changes fastest.
Arguments:
- tokens: bfloat16 [16, 256, 1024], P(None, 'dp', 'col'), parts along dimension 1, may hold values from -6 to 6
- w_input: bfloat16 [2, 1024, 4096], P('layer', None, 'col'), may hold values from -0.1875 to 0.1875
- w_recur: bfloat16 [2, 1024, 4096], P('layer', None, 'col'), may hold values from -0.1875 to 0.1875
- bias: float32 [2, 4096], P('layer', 'col'), may hold values from -1 to 5
Outputs:
- top_states: bfloat16 [16, 256, 1024], P('layer', 'dp', 'col'), parts along dimension 1
- final_h: bfloat16 [2, 256, 1024], P('layer', 'dp', 'col'), parts along dimension 1
- final_c: float32 [2, 256, 1024], P('layer', 'dp', 'col'), parts along dimension 1
There are 2 independent parts, one for each index of `dp`. A program takes and returns all parts, laid end to end along the dimension named above; an argument that names none is the same for every part. Nothing has to cross between parts.
All inputs are finite; a program needn't handle non-finite values.
Results may differ from a plain program's by a relative error of at most 0.008.
Values may be sent and summed in bfloat16 or wider, within the bound.
A program may use at most 64 MiB of HBM per device.

v0:
```python
import jax
import jax.numpy as jnp
from jax import lax
from jax.sharding import PartitionSpec as P


def passed_along(block, axis, distance):
    devices = range(lax.axis_size(axis))
    route = [(i - distance, i) for i in devices if i - distance in devices]
    return lax.ppermute(block, axis, route)


def broadcast(block, axis, source):
    block = jnp.where(lax.axis_index(axis) == source, block, jnp.zeros_like(block))
    return lax.psum(block, axis)


def shards(tokens, w_input, w_recur, bias):
    steps_count, sentences, units = tokens.shape
    w_local = w_input[0]
    r_local = w_recur[0]
    b_local = bias[0]
    layers = lax.axis_size("layer")
    level = lax.axis_index("layer")
    is_first = level == 0
    has_skip = level >= 1
    is_last = level == layers - 1

    def cell_step(gates, cell):
        gates = gates.reshape(sentences, units, 4)
        in_gate = jax.nn.sigmoid(gates[:, :, 0])
        forget = jax.nn.sigmoid(gates[:, :, 1])
        update = jnp.tanh(gates[:, :, 2])
        out_gate = jax.nn.sigmoid(gates[:, :, 3])
        cell_new = forget * cell + in_gate * update
        hidden_new = (out_gate * jnp.tanh(cell_new)).astype(jnp.bfloat16)
        return (hidden_new, cell_new)

    def skip_sum(hidden_new, in_part):
        summed = (hidden_new.astype(jnp.float32) + in_part.astype(jnp.float32)).astype(jnp.bfloat16)
        return jnp.where(has_skip, summed, hidden_new)

    zero_h = jnp.zeros((sentences, units), jnp.bfloat16)
    zero_c = jnp.zeros((sentences, units), jnp.float32)
    buffer = jnp.zeros((steps_count, sentences, units), jnp.bfloat16)
    span = 4
    count = steps_count // span
    block_sections = count + layers - 1
    zero_span = jnp.zeros((span, sentences, units), jnp.bfloat16)

    def section_block(section, carry):
        hidden, cell, outgoing, kept = carry
        which = section - level
        active = (which >= 0) & (which < count)
        first_step = jnp.clip(which, 0, count - 1) * span
        own_tokens = lax.dynamic_slice_in_dim(tokens, first_step, span, 0)
        received = passed_along(outgoing, "layer", 1)
        in_part = jnp.where(is_first, own_tokens, received)
        in_full = lax.all_gather(in_part, "col", axis=2, tiled=True)
        projected = jnp.dot(
            in_full.reshape(span * sentences, in_full.shape[2]),
            w_local,
            preferred_element_type=jnp.float32,
        )
        projected = projected.reshape(span, sentences, w_local.shape[1])
        states = []
        for offset in range(span):
            h_full = lax.all_gather(hidden, "col", axis=1, tiled=True)
            gates = (
                projected[offset]
                + jnp.dot(h_full, r_local, preferred_element_type=jnp.float32)
                + b_local
            )
            hidden_new, cell_new = cell_step(gates, cell)
            hidden = jnp.where(active, hidden_new, hidden)
            cell = jnp.where(active, cell_new, cell)
            states.append(hidden_new)
        produced = jnp.stack(states)
        outgoing = skip_sum(produced, in_part)
        written = lax.dynamic_update_slice_in_dim(kept, produced, first_step, 0)
        kept = jnp.where(active & is_last, written, kept)
        return (hidden, cell, outgoing, kept)

    hidden, cell, outgoing, buffer = lax.fori_loop(
        0, block_sections, section_block, (zero_h, zero_c, zero_span, buffer)
    )
    everything = broadcast(buffer, "layer", layers - 1)
    block = steps_count // layers
    top_states = lax.dynamic_slice_in_dim(everything, level * block, block, 0)
    return (top_states, hidden[None], cell[None])


def solution(mesh):
    in_specs = (
        P(None, "dp", "col"),
        P("layer", None, "col"),
        P("layer", None, "col"),
        P("layer", "col"),
    )
    out_specs = (P("layer", "dp", "col"), P("layer", "dp", "col"), P("layer", "dp", "col"))
    return jax.shard_map(shards, mesh=mesh, in_specs=in_specs, out_specs=out_specs, check_vma=False)
```

profile of v0, /device:TPU:6, one launch (start us, length us, event | category | flops | bytes accessed | tf_op | source)
XLA Modules:
  0.0 718.8 jit_solution(11233482113519952931)
XLA Ops:
  8.2 0.6 copy-done.4
  8.7 670.8 %while.20 = (s32[]{:T(128)}, bf16[128,128]{1,0:T(8,128)(2,1)S(1)}, f32[128,128]{1,0:T(8,128)S(1)}, bf16[4,128,128]{2,1,0:T(8,128)(2,1)S(1)}, bf16[16,128,128]{2,...) while((s32[]{:T(128)}, bf16[128,128]{1,0:T(8,128)(2,1)S(1)}, ...), condition=%wide.region_1.2_spmd.clone, body=%wide.region_0.1_spmd.clone.sunk | while | flops 1076445184 | bytes 28451252 | solution.py:84
  8.7 1.3 collective-permute-start
  10.1 5.8 collective-permute-done
  15.9 1.6 dynamic-slice_select_fusion.2
  17.5 26.8 %all_gather.46 = bf16[128,1024]{1,0:T(8,128)(2,1)S(1)} all-gather(bf16[128,128]{1,0:T(8,128)(2,1)S(1)} %broadcast_select_fusion.18), channel_id=1, replica_groups=mesh['dp'=2,'layer'=2,'col'=8] {'col'}, dimensions={1}, use_global_device_ids=true | all-gather | bytes 294912 | tf_op jit(solution)/shard_map/while/body/eval_jaxpr/all_gather | solution.py:68
  44.3 14.0 %all-gather.2.cloned.1.call-done = bf16[4,128,1024]{2,1,0:T(8,128)(2,1)} async-done(((bf16[4,128,128]{2,1,0:T(8,128)(2,1)}), bf16[4,128,1024]{2,1,0:T(8,128)(2,1)}) %all-gather.2.cloned.1.call-update) | async-done | bytes 1048592 | tf_op jit(solution)/shard_map/while/body/eval_jaxpr/all_gather | solution.py:59
  58.3 2.4 fusion.57
  60.7 0.6 fusion.58
  62.0 24.9 %all_gather.47 = bf16[128,1024]{1,0:T(8,128)(2,1)S(1)} all-gather(bf16[128,128]{1,0:T(8,128)(2,1)S(1)} %get-tuple-element.450), channel_id=1, replica_groups=mesh['dp'=2,'layer'=2,'col'=8] {'col'}, dimensions={1}, use_global_device_ids=true | all-gather | bytes 294912 | tf_op jit(solution)/shard_map/while/body/eval_jaxpr/all_gather | solution.py:68
  86.8 0.6 fusion.60
  88.1 25.7 %all_gather.48 = bf16[128,1024]{1,0:T(8,128)(2,1)S(1)} all-gather(bf16[128,128]{1,0:T(8,128)(2,1)S(1)} %get-tuple-element.456), channel_id=1, replica_groups=mesh['dp'=2,'layer'=2,'col'=8] {'col'}, dimensions={1}, use_global_device_ids=true | all-gather | bytes 294912 | tf_op jit(solution)/shard_map/while/body/eval_jaxpr/all_gather | solution.py:68
  115.0 26.8 %all_gather.49 = bf16[128,1024]{1,0:T(8,128)(2,1)S(1)} all-gather(bf16[128,128]{1,0:T(8,128)(2,1)S(1)} %get-tuple-element.463), channel_id=1, replica_groups=mesh['dp'=2,'layer'=2,'col'=8] {'col'}, dimensions={1}, use_global_device_ids=true | all-gather | bytes 294912 | tf_op jit(solution)/shard_map/while/body/eval_jaxpr/all_gather | solution.py:68
  143.1 0.8 copy-done.1
  144.1 1.3 collective-permute-start
  145.4 5.5 collective-permute-done
  151.0 1.6 dynamic-slice_select_fusion.2
  152.6 26.9 %all_gather.46 = bf16[128,1024]{1,0:T(8,128)(2,1)S(1)} all-gather(bf16[128,128]{1,0:T(8,128)(2,1)S(1)} %broadcast_select_fusion.18), channel_id=1, replica_groups=mesh['dp'=2,'layer'=2,'col'=8] {'col'}, dimensions={1}, use_global_device_ids=true | all-gather | bytes 294912 | tf_op jit(solution)/shard_map/while/body/eval_jaxpr/all_gather | solution.py:68
  179.5 13.1 %all-gather.2.cloned.1.call-done = bf16[4,128,1024]{2,1,0:T(8,128)(2,1)} async-done(((bf16[4,128,128]{2,1,0:T(8,128)(2,1)}), bf16[4,128,1024]{2,1,0:T(8,128)(2,1)}) %all-gather.2.cloned.1.call-update) | async-done | bytes 1048592 | tf_op jit(solution)/shard_map/while/body/eval_jaxpr/all_gather | solution.py:59
  192.6 2.4 fusion.57
  195.0 0.6 fusion.58
  196.3 25.4 %all_gather.47 = bf16[128,1024]{1,0:T(8,128)(2,1)S(1)} all-gather(bf16[128,128]{1,0:T(8,128)(2,1)S(1)} %get-tuple-element.450), channel_id=1, replica_groups=mesh['dp'=2,'layer'=2,'col'=8] {'col'}, dimensions={1}, use_global_device_ids=true | all-gather | bytes 294912 | tf_op jit(solution)/shard_map/while/body/eval_jaxpr/all_gather | solution.py:68
  221.6 0.6 fusion.60
  222.9 24.8 %all_gather.48 = bf16[128,1024]{1,0:T(8,128)(2,1)S(1)} all-gather(bf16[128,128]{1,0:T(8,128)(2,1)S(1)} %get-tuple-element.456), channel_id=1, replica_groups=mesh['dp'=2,'layer'=2,'col'=8] {'col'}, dimensions={1}, use_global_device_ids=true | all-gather | bytes 294912 | tf_op jit(solution)/shard_map/while/body/eval_jaxpr/all_gather | solution.py:68
  248.9 26.7 %all_gather.49 = bf16[128,1024]{1,0:T(8,128)(2,1)S(1)} all-gather(bf16[128,128]{1,0:T(8,128)(2,1)S(1)} %get-tuple-element.463), channel_id=1, replica_groups=mesh['dp'=2,'layer'=2,'col'=8] {'col'}, dimensions={1}, use_global_device_ids=true | all-gather | bytes 294912 | tf_op jit(solution)/shard_map/while/body/eval_jaxpr/all_gather | solution.py:68
  276.9 0.8 copy-done.1
  277.9 1.3 collective-permute-start
  279.3 5.5 collective-permute-done
  284.8 1.6 dynamic-slice_select_fusion.2
  286.4 26.8 %all_gather.46 = bf16[128,1024]{1,0:T(8,128)(2,1)S(1)} all-gather(bf16[128,128]{1,0:T(8,128)(2,1)S(1)} %broadcast_select_fusion.18), channel_id=1, replica_groups=mesh['dp'=2,'layer'=2,'col'=8] {'col'}, dimensions={1}, use_global_device_ids=true | all-gather | bytes 294912 | tf_op jit(solution)/shard_map/while/body/eval_jaxpr/all_gather | solution.py:68
  313.3 13.1 %all-gather.2.cloned.1.call-done = bf16[4,128,1024]{2,1,0:T(8,128)(2,1)} async-done(((bf16[4,128,128]{2,1,0:T(8,128)(2,1)}), bf16[4,128,1024]{2,1,0:T(8,128)(2,1)}) %all-gather.2.cloned.1.call-update) | async-done | bytes 1048592 | tf_op jit(solution)/shard_map/while/body/eval_jaxpr/all_gather | solution.py:59
  326.4 2.4 fusion.57
  328.8 0.6 fusion.58
  330.1 25.4 %all_gather.47 = bf16[128,1024]{1,0:T(8,128)(2,1)S(1)} all-gather(bf16[128,128]{1,0:T(8,128)(2,1)S(1)} %get-tuple-element.450), channel_id=1, replica_groups=mesh['dp'=2,'layer'=2,'col'=8] {'col'}, dimensions={1}, use_global_device_ids=true | all-gather | bytes 294912 | tf_op jit(solution)/shard_map/while/body/eval_jaxpr/all_gather | solution.py:68
  356.7 24.8 %all_gather.48 = bf16[128,1024]{1,0:T(8,128)(2,1)S(1)} all-gather(bf16[128,128]{1,0:T(8,128)(2,1)S(1)} %get-tuple-element.456), channel_id=1, replica_groups=mesh['dp'=2,'layer'=2,'col'=8] {'col'}, dimensions={1}, use_global_device_ids=true | all-gather | bytes 294912 | tf_op jit(solution)/shard_map/while/body/eval_jaxpr/all_gather | solution.py:68
  381.6 0.6 fusion.62
  382.8 26.7 %all_gather.49 = bf16[128,1024]{1,0:T(8,128)(2,1)S(1)} all-gather(bf16[128,128]{1,0:T(8,128)(2,1)S(1)} %get-tuple-element.463), channel_id=1, replica_groups=mesh['dp'=2,'layer'=2,'col'=8] {'col'}, dimensions={1}, use_global_device_ids=true | all-gather | bytes 294912 | tf_op jit(solution)/shard_map/while/body/eval_jaxpr/all_gather | solution.py:68
  410.8 0.8 copy-done.1
  411.8 1.3 collective-permute-start
  413.2 5.5 collective-permute-done
  418.7 1.6 dynamic-slice_select_fusion.2
  420.3 26.7 %all_gather.46 = bf16[128,1024]{1,0:T(8,128)(2,1)S(1)} all-gather(bf16[128,128]{1,0:T(8,128)(2,1)S(1)} %broadcast_select_fusion.18), channel_id=1, replica_groups=mesh['dp'=2,'layer'=2,'col'=8] {'col'}, dimensions={1}, use_global_device_ids=true | all-gather | bytes 294912 | tf_op jit(solution)/shard_map/while/body/eval_jaxpr/all_gather | solution.py:68
  447.0 13.3 %all-gather.2.cloned.1.call-done = bf16[4,128,1024]{2,1,0:T(8,128)(2,1)} async-done(((bf16[4,128,128]{2,1,0:T(8,128)(2,1)}), bf16[4,128,1024]{2,1,0:T(8,128)(2,1)}) %all-gather.2.cloned.1.call-update) | async-done | bytes 1048592 | tf_op jit(solution)/shard_map/while/body/eval_jaxpr/all_gather | solution.py:59
  460.3 2.4 fusion.57
  462.7 0.6 fusion.58
  464.0 25.4 %all_gather.47 = bf16[128,1024]{1,0:T(8,128)(2,1)S(1)} all-gather(bf16[128,128]{1,0:T(8,128)(2,1)S(1)} %get-tuple-element.450), channel_id=1, replica_groups=mesh['dp'=2,'layer'=2,'col'=8] {'col'}, dimensions={1}, use_global_device_ids=true | all-gather | bytes 294912 | tf_op jit(solution)/shard_map/while/body/eval_jaxpr/all_gather | solution.py:68
  489.4 0.6 fusion.60
  490.6 24.8 %all_gather.48 = bf16[128,1024]{1,0:T(8,128)(2,1)S(1)} all-gather(bf16[128,128]{1,0:T(8,128)(2,1)S(1)} %get-tuple-element.456), channel_id=1, replica_groups=mesh['dp'=2,'layer'=2,'col'=8] {'col'}, dimensions={1}, use_global_device_ids=true | all-gather | bytes 294912 | tf_op jit(solution)/shard_map/while/body/eval_jaxpr/all_gather | solution.py:68
  516.7 26.7 %all_gather.49 = bf16[128,1024]{1,0:T(8,128)(2,1)S(1)} all-gather(bf16[128,128]{1,0:T(8,128)(2,1)S(1)} %get-tuple-element.463), channel_id=1, replica_groups=mesh['dp'=2,'layer'=2,'col'=8] {'col'}, dimensions={1}, use_global_device_ids=true | all-gather | bytes 294912 | tf_op jit(solution)/shard_map/while/body/eval_jaxpr/all_gather | solution.py:68
  544.7 0.8 copy-done.1
  545.8 1.3 collective-permute-start
  547.1 5.5 collective-permute-done
  552.6 1.6 dynamic-slice_select_fusion.2
  554.2 26.7 %all_gather.46 = bf16[128,1024]{1,0:T(8,128)(2,1)S(1)} all-gather(bf16[128,128]{1,0:T(8,128)(2,1)S(1)} %broadcast_select_fusion.18), channel_id=1, replica_groups=mesh['dp'=2,'layer'=2,'col'=8] {'col'}, dimensions={1}, use_global_device_ids=true | all-gather | bytes 294912 | tf_op jit(solution)/shard_map/while/body/eval_jaxpr/all_gather | solution.py:68
  580.9 13.3 %all-gather.2.cloned.1.call-done = bf16[4,128,1024]{2,1,0:T(8,128)(2,1)} async-done(((bf16[4,128,128]{2,1,0:T(8,128)(2,1)}), bf16[4,128,1024]{2,1,0:T(8,128)(2,1)}) %all-gather.2.cloned.1.call-update) | async-done | bytes 1048592 | tf_op jit(solution)/shard_map/while/body/eval_jaxpr/all_gather | solution.py:59
  594.2 2.4 fusion.57
  596.6 0.6 fusion.58
  597.9 25.4 %all_gather.47 = bf16[128,1024]{1,0:T(8,128)(2,1)S(1)} all-gather(bf16[128,128]{1,0:T(8,128)(2,1)S(1)} %get-tuple-element.450), channel_id=1, replica_groups=mesh['dp'=2,'layer'=2,'col'=8] {'col'}, dimensions={1}, use_global_device_ids=true | all-gather | bytes 294912 | tf_op jit(solution)/shard_map/while/body/eval_jaxpr/all_gather | solution.py:68
  624.6 24.7 %all_gather.48 = bf16[128,1024]{1,0:T(8,128)(2,1)S(1)} all-gather(bf16[128,128]{1,0:T(8,128)(2,1)S(1)} %get-tuple-element.456), channel_id=1, replica_groups=mesh['dp'=2,'layer'=2,'col'=8] {'col'}, dimensions={1}, use_global_device_ids=true | all-gather | bytes 294912 | tf_op jit(solution)/shard_map/while/body/eval_jaxpr/all_gather | solution.py:68
  650.6 26.7 %all_gather.49 = bf16[128,1024]{1,0:T(8,128)(2,1)S(1)} all-gather(bf16[128,128]{1,0:T(8,128)(2,1)S(1)} %get-tuple-element.463), channel_id=1, replica_groups=mesh['dp'=2,'layer'=2,'col'=8] {'col'}, dimensions={1}, use_global_device_ids=true | all-gather | bytes 294912 | tf_op jit(solution)/shard_map/while/body/eval_jaxpr/all_gather | solution.py:68
  678.6 0.8 copy-done.1
  679.6 0.8 broadcast_select_fusion.9
  680.5 29.5 %all-reduce.2.cloned.1.call-done = bf16[16,128,128]{2,1,0:T(8,128)(2,1)} async-done(((bf16[16,128,128]{2,1,0:T(8,128)(2,1)}), bf16[16,128,128]{2,1,0:T(8,128)(2,1)}) %all-reduce.2.cloned.1.call-update) | async-done | bytes 524304 | tf_op jit(solution)/shard_map/psum | solution.py:15
  710.0 1.7 constant_dynamic-slice_fusion
  (187 shorter events, 20.2 us)
Async XLA Ops:
  8.0 0.7 copy-start.4
  8.7 49.6 %all-gather.2.cloned.1.call-start = ((), (), s32[]{:S(2)}) async-start(), calls=%async_computation.1 | async-start | bytes 1179648 | tf_op jit(solution)/shard_map/while/body/eval_jaxpr/all_gather | solution.py:59
  8.7 7.1 collective-permute-start
  58.3 2.4 copy-start
  143.0 0.9 copy-start.1
  144.1 48.6 %all-gather.2.cloned.1.call-start = ((), (), s32[]{:S(2)}) async-start(), calls=%async_computation.1 | async-start | bytes 1179648 | tf_op jit(solution)/shard_map/while/body/eval_jaxpr/all_gather | solution.py:59
  144.1 6.9 collective-permute-start
  192.6 2.4 copy-start
  276.8 0.9 copy-start.1
  277.9 48.6 %all-gather.2.cloned.1.call-start = ((), (), s32[]{:S(2)}) async-start(), calls=%async_computation.1 | async-start | bytes 1179648 | tf_op jit(solution)/shard_map/while/body/eval_jaxpr/all_gather | solution.py:59
  277.9 6.9 collective-permute-start
  326.4 2.4 copy-start
  410.7 0.9 copy-start.1
  411.8 48.6 %all-gather.2.cloned.1.call-start = ((), (), s32[]{:S(2)}) async-start(), calls=%async_computation.1 | async-start | bytes 1179648 | tf_op jit(solution)/shard_map/while/body/eval_jaxpr/all_gather | solution.py:59
  411.8 6.9 collective-permute-start
  460.3 2.4 copy-start
  544.7 0.9 copy-start.1
  545.7 48.6 %all-gather.2.cloned.1.call-start = ((), (), s32[]{:S(2)}) async-start(), calls=%async_computation.1 | async-start | bytes 1179648 | tf_op jit(solution)/shard_map/while/body/eval_jaxpr/all_gather | solution.py:59
  545.8 6.9 collective-permute-start
  594.2 2.4 copy-start
  678.5 0.9 copy-start.1
  679.5 0.9 copy-start.2
  679.5 0.9 copy-start.3
  679.5 30.4 %all-reduce.2.cloned.1.call-start = ((), (), s32[]{:S(2)}) async-start(), calls=%async_computation | async-start | bytes 1048576 | tf_op jit(solution)/shard_map/psum | solution.py:15
Sparse Core Ops, SparseCore 0:
  17.6 40.6 all-gather.1
  152.7 39.8 all-gather.1
  286.5 39.8 all-gather.1
  420.4 39.8 all-gather.1
  554.3 39.8 all-gather.1
Sparse Core Ops, SparseCore 1:
  682.3 27.6 all-reduce.1
where the time goes:
time: 722 us; the launch traced here: 719 us
  blocking collectives  519 us (72%)
  waiting for transfers between devices  124 us (17%)
  matrix products  23.1 us (3%)
  local copies, waits for them, and re-layouts  17.6 us (2%)
  between operations  15.2 us (2%)
  other arithmetic  11.2 us (2%)
    all_gather x20, blocking collectives, section_block(): h_full = lax.all_gather(hidden, 'col', axis=1, tiled=True)  519 us
    all_gather x5, waiting for transfers between devices, section_block(): in_full = lax.all_gather(in_part, 'col', axis=2, tiled=True)  66.9 us
    psum x1, waiting for transfers between devices, broadcast(): return lax.psum(block, axis)  29.5 us
    ppermute x5, waiting for transfers between devices, passed_along(): return lax.ppermute(block, axis, route)  28 us
  transfers between devices with their start and end apart: 11, of which 11 were waited for; matrix products, arithmetic and copies ran while one was open for 0% of the time, Pallas kernels for 0%

commit v1 on v0

--- a/solution.py
+++ b/solution.py
@@ -1,6 +1,10 @@
+import functools
+
 import jax
 import jax.numpy as jnp
 from jax import lax
+from jax.experimental import pallas as pl
+from jax.experimental.pallas import tpu as pltpu
 from jax.sharding import PartitionSpec as P
 
 
@@ -90,6 +94,338 @@
     return (top_states, hidden[None], cell[None])
 
 
+MESH = pl.DeviceIdType.MESH
+CHUNK = 4
+
+
+def lstm_kernel(
+    groups,
+    tokens, w_in, w_rec, bias,
+    top, final_h, final_c,
+    xs, hs, wi, wr, raw_in, raw_rec, braw, bperm, cell, gates,
+    send_sem, x_sem, h_sem, tok_y_sem, tok_z_sem, w_y_sem, w_d_sem, b_sem, top_sem, fin_sem,
+):
+    steps, sentences, units = tokens.shape
+    half = sentences // 2
+    depth = w_in.shape[0]
+    part_rows = depth // 2
+    chunks = steps // CHUNK
+    keep = steps // 2
+    dp = lax.axis_index("dp")
+    level = lax.axis_index("layer")
+    col = lax.axis_index("col")
+    p = col // 2
+    q = lax.rem(col, 2)
+    other = 1 - q
+    pair = {"col": 2 * p + other}
+    twin = {"dp": 1 - dp}
+    is_first = level == 0
+    is_last = level == 1
+
+    def copy(src, dst, sem, device):
+        return pltpu.make_async_remote_copy(
+            src_ref=src, dst_ref=dst, send_sem=send_sem, recv_sem=sem,
+            device_id=device, device_id_type=MESH,
+        )
+
+    def near(i):
+        return lax.rem(p + i, groups)
+
+    barrier = pltpu.get_barrier_semaphore()
+    targets = [{"col": 2 * near(i) + q} for i in range(1, groups)]
+    targets += [pair, twin]
+    targets += [{"layer": 1 - level, "col": 2 * near(i) + q} for i in range(groups)]
+    targets += [{"layer": 1 - level, "col": 2 * p + other}]
+    for device in targets:
+        pl.semaphore_signal(barrier, inc=1, device_id=device, device_id_type=MESH)
+    pl.semaphore_wait(barrier, len(targets))
+
+    my_rows = pl.ds(pl.multiple_of(q * half, half), half)
+    other_rows = pl.ds(pl.multiple_of(other * half, half), half)
+
+    def span(c):
+        return pl.ds(c * CHUNK, CHUNK)
+
+    def tok_to_pair(c):
+        return copy(tokens.at[span(c), other_rows], xs.at[span(c), p, q], tok_y_sem.at[c], pair)
+
+    def tok_from_pair(c):
+        place = xs.at[span(c), p, other]
+        return copy(place, place, tok_y_sem.at[c], pair)
+
+    def tok_own(c, i):
+        return copy(tokens.at[span(c), my_rows], xs.at[span(c), p, q], tok_z_sem.at[c, p, q], {"col": 2 * near(i) + q})
+
+    def tok_forward(c, i):
+        place = xs.at[span(c), p, other]
+        return copy(place, place, tok_z_sem.at[c, p, other], {"col": 2 * near(i) + q})
+
+    def tok_arrived(c, i, y):
+        place = xs.at[span(c), near(i), y]
+        return copy(place, place, tok_z_sem.at[c, near(i), y], pair)
+
+    part = pl.ds(pl.multiple_of(dp * part_rows, part_rows), part_rows)
+    twin_part = pl.ds(pl.multiple_of((1 - dp) * part_rows, part_rows), part_rows)
+    weights = ((w_in, raw_in), (w_rec, raw_rec))
+
+    def w_to_pair(k):
+        own, raw = weights[k]
+        return copy(own.at[part], raw.at[part], w_y_sem.at[k], pair)
+
+    def w_to_twin(k):
+        raw = weights[k][1]
+        return copy(raw.at[part], raw.at[part], w_d_sem.at[k], twin)
+
+    def w_from_twin(k):
+        raw = weights[k][1]
+        return copy(raw.at[twin_part], raw.at[twin_part], w_d_sem.at[k], twin)
+
+    bias_copy = copy(bias, braw, b_sem, pair)
+
+    @pl.when(is_first)
+    def _():
+        tok_to_pair(0).start()
+        for i in range(1, groups):
+            tok_own(0, i).start()
+
+    bias_copy.start()
+    w_to_pair(0).start()
+    w_to_pair(1).start()
+
+    @pl.when(is_first)
+    def _():
+        for c in range(1, chunks):
+            tok_to_pair(c).start()
+        for t in range(steps):
+            xs[t, p, q] = tokens[t, my_rows]
+
+    cell[...] = jnp.zeros_like(cell)
+    width = 4 * units
+    row = lax.broadcasted_iota(jnp.int32, (width, width), 0)
+    column = lax.broadcasted_iota(jnp.int32, (width, width), 1)
+    spread = row == 4 * lax.rem(column, units) + column // units
+    order = jnp.where(spread, 1.0, 0.0).astype(jnp.bfloat16)
+    block_rows = 256
+
+    def regroup(src, dst, which):
+        @pl.loop(0, depth // block_rows)
+        def _(r):
+            rows = pl.ds(pl.multiple_of(r * block_rows, block_rows), block_rows)
+            moved = jnp.dot(src[rows], order, preferred_element_type=jnp.float32)
+            dst[which, rows] = moved.astype(jnp.bfloat16)
+
+    def regroup_bias(src, which):
+        value = jnp.broadcast_to(src[...], (8, width))
+        total = jnp.zeros((8, width), jnp.float32)
+        for _ in range(3):
+            piece = value.astype(jnp.bfloat16)
+            total = total + jnp.dot(piece, order, preferred_element_type=jnp.float32)
+            value = value - piece.astype(jnp.float32)
+        bperm[which] = total
+
+    regroup(w_in, wi, q)
+    regroup_bias(bias, q)
+
+    @pl.when(is_first)
+    def _():
+        tok_from_pair(0).wait_recv()
+        for i in range(1, groups):
+            tok_forward(0, i).start()
+
+    regroup(w_rec, wr, q)
+    bias_copy.wait_recv()
+    regroup_bias(braw, other)
+    w_to_pair(0).wait_recv()
+    w_to_twin(0).start()
+    w_from_twin(0).wait_recv()
+    regroup(raw_in, wi, other)
+
+    def to_peer(t, i):
+        return copy(hs.at[t, p], hs.at[t, p], h_sem.at[t, p], {"col": 2 * near(i) + q})
+
+    def from_peer(t, i):
+        return copy(hs.at[t, near(i)], hs.at[t, near(i)], h_sem.at[t, near(i)], pair)
+
+    def to_next(t, i):
+        return copy(hs.at[t, p], xs.at[t, p], x_sem.at[t, p], {"layer": 1 - level, "col": 2 * near(i) + q})
+
+    def from_before(t, i):
+        return copy(xs.at[t, near(i)], xs.at[t, near(i)], x_sem.at[t, near(i)], pair)
+
+    def joined(ref, t):
+        return jnp.concatenate([ref[t, g, y] for g in range(groups) for y in range(2)], axis=1)
+
+    def top_far(t, b):
+        return copy(hs.at[t, p, b], top.at[t, my_rows], top_sem.at[t, q], {"layer": 1 - level, "col": 2 * p + b})
+
+    def top_pair(t):
+        return copy(hs.at[t, p, other], top.at[t - keep, my_rows], top_sem.at[t - keep, q], pair)
+
+    @pl.loop(0, steps)
+    def _(t):
+        @pl.when(is_first & (lax.rem(t, CHUNK) == 0))
+        def _():
+            c = t // CHUNK
+            for i in range(1, groups):
+                tok_arrived(c, i, 0).wait_recv()
+                tok_arrived(c, i, 1).wait_recv()
+
+        @pl.when(is_last)
+        def _():
+            for i in range(groups):
+                from_before(t, i).wait_recv()
+
+        given = joined(xs, t)
+        for b in range(2):
+            gates[b] = jnp.dot(given, wi[b], preferred_element_type=jnp.float32) + bperm[b, 0:1]
+
+        @pl.when(t == 1)
+        def _():
+            w_to_pair(1).wait_recv()
+            w_to_twin(1).start()
+            w_from_twin(1).wait_recv()
+            regroup(raw_rec, wr, other)
+
+        @pl.when(t > 0)
+        def _():
+            for i in range(1, groups):
+                from_peer(t - 1, i).wait_recv()
+            state = joined(hs, t - 1)
+            for b in range(2):
+                gates[b] += jnp.dot(state, wr[b], preferred_element_type=jnp.float32)
+
+        for b in range(2):
+            in_gate = 0.5 * jnp.tanh(0.5 * gates[b, :, 0:units]) + 0.5
+            forget = 0.5 * jnp.tanh(0.5 * gates[b, :, units : 2 * units]) + 0.5
+            update = jnp.tanh(gates[b, :, 2 * units : 3 * units])
+            out_gate = 0.5 * jnp.tanh(0.5 * gates[b, :, 3 * units :]) + 0.5
+            cell_new = forget * cell[b] + in_gate * update
+            cell[b] = cell_new
+            hs[t, p, b] = (out_gate * jnp.tanh(cell_new)).astype(jnp.bfloat16)
+
+        @pl.when(t < steps - 1)
+        def _():
+            for i in range(1, groups):
+                to_peer(t, i).start()
+
+        @pl.when(is_first)
+        def _():
+            for i in range(groups):
+                to_next(t, i).start()
+
+            @pl.when((lax.rem(t, CHUNK) == 1) & (t < steps - CHUNK))
+            def _():
+                c = t // CHUNK + 1
+                tok_from_pair(c).wait_recv()
+                for i in range(1, groups):
+                    tok_own(c, i).start()
+                    tok_forward(c, i).start()
+
+        @pl.when(is_last & (t < keep))
+        def _():
+            top_far(t, 0).start()
+            top_far(t, 1).start()
+
+        @pl.when(is_last & (t >= keep))
+        def _():
+            top_pair(t).start()
+            top[t - keep, my_rows] = hs[t, p, q]
+
+    end = steps - 1
+    fin_h = copy(hs.at[end, p, other], final_h.at[0, my_rows], fin_sem.at[0], pair)
+    fin_c = copy(cell.at[other], final_c.at[0, my_rows], fin_sem.at[1], pair)
+    fin_h.start()
+    fin_c.start()
+    final_h[0, my_rows] = hs[end, p, q]
+    final_c[0, my_rows] = cell[q]
+
+    bias_copy.wait_send()
+    for k in range(2):
+        w_to_pair(k).wait_send()
+        w_to_twin(k).wait_send()
+    fin_h.wait()
+    fin_c.wait()
+
+    @pl.loop(0, end)
+    def _(t):
+        for i in range(1, groups):
+            to_peer(t, i).wait_send()
+
+    @pl.when(is_first)
+    def _():
+        for c in range(chunks):
+            tok_to_pair(c).wait_send()
+            for i in range(1, groups):
+                tok_own(c, i).wait_send()
+                tok_forward(c, i).wait_send()
+
+        @pl.loop(0, steps)
+        def _(t):
+            for i in range(groups):
+                to_next(t, i).wait_send()
+
+        @pl.loop(0, keep)
+        def _(t):
+            for y in range(2):
+                rows = top.at[t, pl.ds(y * half, half)]
+                copy(rows, rows, top_sem.at[t, y], pair).wait_recv()
+
+    @pl.when(is_last)
+    def _():
+        @pl.loop(0, keep)
+        def _(t):
+            top_far(t, 0).wait_send()
+            top_far(t, 1).wait_send()
+            top_pair(t + keep).wait_send()
+            rows = top.at[t, other_rows]
+            copy(rows, rows, top_sem.at[t, other], pair).wait_recv()
+
+
+def fused(tokens, w_input, w_recur, bias):
+    steps, sentences, units = tokens.shape
+    depth, width = w_input.shape[1:]
+    groups = lax.axis_size("col") // 2
+    half = sentences // 2
+    bf16, f32, dma = jnp.bfloat16, jnp.float32, pltpu.SemaphoreType.DMA
+    vmem = pl.BlockSpec(memory_space=pltpu.VMEM)
+    return pl.pallas_call(
+        functools.partial(lstm_kernel, groups),
+        out_shape=(
+            jax.ShapeDtypeStruct((steps // 2, sentences, units), bf16),
+            jax.ShapeDtypeStruct((1, sentences, units), bf16),
+            jax.ShapeDtypeStruct((1, sentences, units), f32),
+        ),
+        in_specs=[vmem] * 4,
+        out_specs=(vmem, vmem, vmem),
+        scratch_shapes=[
+            pltpu.VMEM((steps, groups, 2, half, units), bf16),
+            pltpu.VMEM((steps, groups, 2, half, units), bf16),
+            pltpu.VMEM((2, depth, width), bf16),
+            pltpu.VMEM((2, depth, width), bf16),
+            pltpu.VMEM((depth, width), bf16),
+            pltpu.VMEM((depth, width), bf16),
+            pltpu.VMEM((1, width), f32),
+            pltpu.VMEM((2, 8, width), f32),
+            pltpu.VMEM((2, half, units), f32),
+            pltpu.VMEM((2, half, width), f32),
+            dma,
+            dma((steps, groups)),
+            dma((steps, groups)),
+            dma((steps // CHUNK,)),
+            dma((steps // CHUNK, groups, 2)),
+            dma((2,)),
+            dma((2,)),
+            dma,
+            dma((steps // 2, 2)),
+            dma((2,)),
+        ],
+        compiler_params=pltpu.CompilerParams(
+            collective_id=0, has_side_effects=True, vmem_limit_bytes=48 * 2**20
+        ),
+        name="lstm",
+    )(tokens, w_input[0], w_recur[0], bias)
+
+
 def solution(mesh):
     in_specs = (
         P(None, "dp", "col"),
@@ -98,4 +434,12 @@
         P("layer", "col"),
     )
     out_specs = (P("layer", "dp", "col"), P("layer", "dp", "col"), P("layer", "dp", "col"))
-    return jax.shard_map(shards, mesh=mesh, in_specs=in_specs, out_specs=out_specs, check_vma=False)
+    cols = mesh.shape["col"]
+
+    def body(tokens, w_input, w_recur, bias):
+        steps, sentences, units = tokens.shape
+        fits = mesh.shape["layer"] == 2 and mesh.shape["dp"] == 2 and cols % 2 == 0
+        fits = fits and units % 128 == 0 and sentences % 32 == 0 and steps % CHUNK == 0
+        return (fused if fits else shards)(tokens, w_input, w_recur, bias)
+
+    return jax.shard_map(body, mesh=mesh, in_specs=in_specs, out_specs=out_specs, check_vma=False)

time: 722 us -> 169 us (0.23)
  blocking collectives: 519 us -> 0 us
  Pallas kernels: 0 us -> 162 us
  waiting for transfers between devices: 124 us -> 0 us
  matrix products: 23.1 us -> 0 us
  between operations: 15.2 us -> 0.65 us
  local copies, waits for them, and re-layouts: 17.6 us -> 6.11 us
  other arithmetic: 11.2 us -> 0 us
    all_gather x20 -> x0, blocking collectives: 519 us -> none  [section_block(): h_full = lax.all_gather(hidden, 'col', axis=1, tiled=True)]
    pallas_call x0 -> x1, Pallas kernels: none -> 162 us  [fused(): pl.pallas_call(functools.partial(lstm_kernel, groups), out_shape=(jax.Sha...]
    all_gather x5 -> x0, waiting for transfers between devices: 66.9 us -> none  [section_block(): in_full = lax.all_gather(in_part, 'col', axis=2, tiled=True)]
    psum x1 -> x0, waiting for transfers between devices: 29.5 us -> none  [broadcast(): return lax.psum(block, axis)]
    ppermute x5 -> x0, waiting for transfers between devices: 28 us -> none  [passed_along(): return lax.ppermute(block, axis, route)]
    dot_general x25 -> x0, matrix products: 23.1 us -> none  [the longest x5 11.9 us: section_block(): jnp.dot(in_full.reshape(span * sentences, in_full.shape[2]), w_local, pre...]
    while x100 -> x0, local copies, waits for them, and re-layouts: 11.6 us -> none
    select_n x36 -> x0, other arithmetic: 11.1 us -> none  [the longest x5 7.87 us: section_block(): in_part = jnp.where(is_first, own_tokens, received)]
  transfers between devices with their start and end apart: 11 -> 0, of which waited for: 11 -> 0; matrix products, arithmetic and copies ran while one was open for 0% -> 0% of each run, Pallas kernels for 0% -> 0%
where the time goes in v1:
time: 169 us; the launch traced here: 168 us
  Pallas kernels  162 us (96%)
  local copies, waits for them, and re-layouts  6.11 us (4%)
    pallas_call x1, Pallas kernels, fused(): pl.pallas_call(functools.partial(lstm_kernel, groups), out_shape=(jax.Sha...  162 us
    unnamed x11, local copies, waits for them, and re-layouts  6.11 us

profile of v1, /device:TPU:6, one launch (start us, length us, event | category | flops | bytes accessed | tf_op | source)
XLA Modules:
  0.0 168.5 jit_solution(12547893584197268048)
XLA Ops:
  0.6 0.0 copy-start.3
  0.6 0.7 copy-done.3
  1.3 0.0 copy-start
  1.3 1.2 copy-done
  2.5 0.0 copy-start.1
  2.5 1.2 copy-done.1
  3.8 0.0 copy-start.2
  3.8 1.0 copy-done.2
  4.8 161.7 %lstm.1 = (bf16[8,128,128]{2,1,0:T(8,128)(2,1)S(1)}, bf16[1,128,128]{2,1,0:T(8,128)(2,1)S(1)}, f32[1,128,128]{2,1,0:T(8,128)S(1)}) custom-call(bf16[16,128,128]{2,1,0:T(8,128)(2,1)S(1)} %copy-done.2, bf16[1024,512]{1,0:T(8,128)(2,1)S(1)} %bitcast.2, bf16[1024,512]{1,0:T(8,128)(2,1)S(1)} %bitcast.3, f32[1,512]{1,0:T(1,128)S(1)} %copy-done.3), custom_call_target="tpu_custom_call" | custom-call | tf_op jit(solution)/shard_map/lstm/pallas_call | solution.py:391
  166.5 0.7 copy.10
  167.2 0.6 copy.11
  167.8 0.6 copy.12
Async XLA Ops:
  0.6 0.7 copy-start.3
  1.3 1.2 copy-start
  2.5 1.2 copy-start.1
  3.8 1.0 copy-start.2

commit v2 on v1

--- a/solution.py
+++ b/solution.py
@@ -102,15 +102,16 @@
     groups,
     tokens, w_in, w_rec, bias,
     top, final_h, final_c,
-    xs, hs, wi, wr, raw_in, raw_rec, braw, bperm, cell, gates,
-    send_sem, x_sem, h_sem, tok_y_sem, tok_z_sem, w_y_sem, w_d_sem, b_sem, top_sem, fin_sem,
+    xs, hs, ts, wi, wr, own_in, own_rec, raw_in, raw_rec, braw, bperm, cell, gates,
+    send_sem, x_sem, h_sem, tok_y_sem, tok_z_sem, tok_x_sem, tok_own_sem,
+    w_own_sem, w_y_sem, w_d_sem, b_sem, top_sem, fin_sem,
 ):
     steps, sentences, units = tokens.shape
     half = sentences // 2
     depth = w_in.shape[0]
     part_rows = depth // 2
-    chunks = steps // CHUNK
     keep = steps // 2
+    chunks = keep // CHUNK
     dp = lax.axis_index("dp")
     level = lax.axis_index("layer")
     col = lax.axis_index("col")
@@ -134,8 +135,7 @@
     barrier = pltpu.get_barrier_semaphore()
     targets = [{"col": 2 * near(i) + q} for i in range(1, groups)]
     targets += [pair, twin]
-    targets += [{"layer": 1 - level, "col": 2 * near(i) + q} for i in range(groups)]
-    targets += [{"layer": 1 - level, "col": 2 * p + other}]
+    targets += [{"layer": 1 - level, "col": 2 * p + y} for y in range(2)]
     for device in targets:
         pl.semaphore_signal(barrier, inc=1, device_id=device, device_id_type=MESH)
     pl.semaphore_wait(barrier, len(targets))
@@ -146,23 +146,37 @@
     def span(c):
         return pl.ds(c * CHUNK, CHUNK)
 
-    def tok_to_pair(c):
-        return copy(tokens.at[span(c), other_rows], xs.at[span(c), p, q], tok_y_sem.at[c], pair)
-
-    def tok_from_pair(c):
-        place = xs.at[span(c), p, other]
+    def source(c):
+        return pl.ds(level * keep + c * CHUNK, CHUNK)
+
+    def tok_local(buf, c):
+        return pltpu.make_async_copy(tokens.at[source(c), my_rows], buf.at[span(c), p, q], tok_own_sem.at[c])
+
+    def tok_to_pair(buf, c):
+        return copy(tokens.at[source(c), other_rows], buf.at[span(c), p, q], tok_y_sem.at[c], pair)
+
+    def tok_from_pair(buf, c):
+        place = buf.at[span(c), p, other]
         return copy(place, place, tok_y_sem.at[c], pair)
 
-    def tok_own(c, i):
-        return copy(tokens.at[span(c), my_rows], xs.at[span(c), p, q], tok_z_sem.at[c, p, q], {"col": 2 * near(i) + q})
-
-    def tok_forward(c, i):
-        place = xs.at[span(c), p, other]
+    def tok_own(buf, c, i):
+        return copy(tokens.at[source(c), my_rows], buf.at[span(c), p, q], tok_z_sem.at[c, p, q], {"col": 2 * near(i) + q})
+
+    def tok_forward(buf, c, i):
+        place = buf.at[span(c), p, other]
         return copy(place, place, tok_z_sem.at[c, p, other], {"col": 2 * near(i) + q})
 
-    def tok_arrived(c, i, y):
-        place = xs.at[span(c), near(i), y]
+    def tok_arrived(buf, c, i, y):
+        place = buf.at[span(c), near(i), y]
         return copy(place, place, tok_z_sem.at[c, near(i), y], pair)
+
+    def tok_over(c):
+        return copy(ts.at[span(c)], xs.at[pl.ds(keep + c * CHUNK, CHUNK)], tok_x_sem.at[c], {"layer": 1 - level})
+
+    def tok_all(buf, c):
+        for i in range(1, groups):
+            tok_arrived(buf, c, i, 0).wait_recv()
+            tok_arrived(buf, c, i, 1).wait_recv()
 
     part = pl.ds(pl.multiple_of(dp * part_rows, part_rows), part_rows)
     twin_part = pl.ds(pl.multiple_of((1 - dp) * part_rows, part_rows), part_rows)
@@ -182,22 +196,40 @@
 
     bias_copy = copy(bias, braw, b_sem, pair)
 
+    def own_weights(k):
+        return pltpu.make_async_copy(weights[k][0], (own_in, own_rec)[k], w_own_sem.at[k])
+
     @pl.when(is_first)
     def _():
-        tok_to_pair(0).start()
-        for i in range(1, groups):
-            tok_own(0, i).start()
-
+        tok_to_pair(xs, 0).start()
+        for i in range(1, groups):
+            tok_own(xs, 0, i).start()
+
+    @pl.when(is_last)
+    def _():
+        for c in range(chunks):
+            tok_to_pair(ts, c).start()
+        for i in range(1, groups):
+            tok_own(ts, 0, i).start()
+
+    own_weights(0).start()
     bias_copy.start()
     w_to_pair(0).start()
+
+    @pl.when(is_first)
+    def _():
+        for c in range(1, chunks):
+            tok_to_pair(xs, c).start()
+        for c in range(chunks):
+            tok_local(xs, c).start()
+
+    @pl.when(is_last)
+    def _():
+        for c in range(chunks):
+            tok_local(ts, c).start()
+
+    own_weights(1).start()
     w_to_pair(1).start()
-
-    @pl.when(is_first)
-    def _():
-        for c in range(1, chunks):
-            tok_to_pair(c).start()
-        for t in range(steps):
-            xs[t, p, q] = tokens[t, my_rows]
 
     cell[...] = jnp.zeros_like(cell)
     width = 4 * units
@@ -223,16 +255,34 @@
             value = value - piece.astype(jnp.float32)
         bperm[which] = total
 
-    regroup(w_in, wi, q)
+    own_weights(0).wait()
+    regroup(own_in, wi, q)
     regroup_bias(bias, q)
 
+    def hand_on(buf):
+        for c in range(chunks):
+            tok_from_pair(buf, c).wait_recv()
+            for i in range(1, groups):
+                tok_forward(buf, c, i).start()
+            if c + 1 < chunks:
+                for i in range(1, groups):
+                    tok_own(buf, c + 1, i).start()
+
+    @pl.when(is_last)
+    def _():
+        hand_on(ts)
+
     @pl.when(is_first)
     def _():
-        tok_from_pair(0).wait_recv()
-        for i in range(1, groups):
-            tok_forward(0, i).start()
-
-    regroup(w_rec, wr, q)
+        tok_from_pair(xs, 0).wait_recv()
+        for i in range(1, groups):
+            tok_forward(xs, 0, i).start()
+        for c in range(1, chunks):
+            for i in range(1, groups):
+                tok_own(xs, c, i).start()
+
+    own_weights(1).wait()
+    regroup(own_rec, wr, q)
     bias_copy.wait_recv()
     regroup_bias(braw, other)
     w_to_pair(0).wait_recv()
@@ -240,17 +290,28 @@
     w_from_twin(0).wait_recv()
     regroup(raw_in, wi, other)
 
+    @pl.when(is_first)
+    def _():
+        for c in range(1, chunks):
+            tok_from_pair(xs, c).wait_recv()
+            for i in range(1, groups):
+                tok_forward(xs, c, i).start()
+
+    @pl.when(is_last)
+    def _():
+        for c in range(chunks):
+            tok_local(ts, c).wait()
+            tok_all(ts, c)
+            tok_over(c).start()
+
     def to_peer(t, i):
         return copy(hs.at[t, p], hs.at[t, p], h_sem.at[t, p], {"col": 2 * near(i) + q})
 
     def from_peer(t, i):
         return copy(hs.at[t, near(i)], hs.at[t, near(i)], h_sem.at[t, near(i)], pair)
 
-    def to_next(t, i):
-        return copy(hs.at[t, p], xs.at[t, p], x_sem.at[t, p], {"layer": 1 - level, "col": 2 * near(i) + q})
-
-    def from_before(t, i):
-        return copy(xs.at[t, near(i)], xs.at[t, near(i)], x_sem.at[t, near(i)], pair)
+    def to_next(t, g):
+        return copy(hs.at[t, g], xs.at[t, g], x_sem.at[t, g], {"layer": 1 - level})
 
     def joined(ref, t):
         return jnp.concatenate([ref[t, g, y] for g in range(groups) for y in range(2)], axis=1)
@@ -260,20 +321,34 @@
 
     def top_pair(t):
         return copy(hs.at[t, p, other], top.at[t - keep, my_rows], top_sem.at[t - keep, q], pair)
+
+    def peers_in(t):
+        for i in range(1, groups):
+            from_peer(t, i).wait_recv()
+
+            @pl.when(is_first)
+            def _():
+                to_next(t, near(i)).start()
 
     @pl.loop(0, steps)
     def _(t):
         @pl.when(is_first & (lax.rem(t, CHUNK) == 0))
         def _():
-            c = t // CHUNK
-            for i in range(1, groups):
-                tok_arrived(c, i, 0).wait_recv()
-                tok_arrived(c, i, 1).wait_recv()
+            c = lax.rem(t // CHUNK, chunks)
+
+            @pl.when(t < keep)
+            def _():
+                tok_local(xs, c).wait()
+                tok_all(xs, c)
+
+            @pl.when(t >= keep)
+            def _():
+                tok_over(c).wait_recv()
 
         @pl.when(is_last)
         def _():
-            for i in range(groups):
-                from_before(t, i).wait_recv()
+            for g in range(groups):
+                to_next(t, g).wait_recv()
 
         given = joined(xs, t)
         for b in range(2):
@@ -288,8 +363,7 @@
 
         @pl.when(t > 0)
         def _():
-            for i in range(1, groups):
-                from_peer(t - 1, i).wait_recv()
+            peers_in(t - 1)
             state = joined(hs, t - 1)
             for b in range(2):
                 gates[b] += jnp.dot(state, wr[b], preferred_element_type=jnp.float32)
@@ -303,23 +377,14 @@
             cell[b] = cell_new
             hs[t, p, b] = (out_gate * jnp.tanh(cell_new)).astype(jnp.bfloat16)
 
-        @pl.when(t < steps - 1)
+        @pl.when(is_first | (t < steps - 1))
         def _():
             for i in range(1, groups):
                 to_peer(t, i).start()
 
         @pl.when(is_first)
         def _():
-            for i in range(groups):
-                to_next(t, i).start()
-
-            @pl.when((lax.rem(t, CHUNK) == 1) & (t < steps - CHUNK))
-            def _():
-                c = t // CHUNK + 1
-                tok_from_pair(c).wait_recv()
-                for i in range(1, groups):
-                    tok_own(c, i).start()
-                    tok_forward(c, i).start()
+            to_next(t, p).start()
 
         @pl.when(is_last & (t < keep))
         def _():
@@ -332,6 +397,11 @@
             top[t - keep, my_rows] = hs[t, p, q]
 
     end = steps - 1
+
+    @pl.when(is_first)
+    def _():
+        peers_in(end)
+
     fin_h = copy(hs.at[end, p, other], final_h.at[0, my_rows], fin_sem.at[0], pair)
     fin_c = copy(cell.at[other], final_c.at[0, my_rows], fin_sem.at[1], pair)
     fin_h.start()
@@ -351,18 +421,23 @@
         for i in range(1, groups):
             to_peer(t, i).wait_send()
 
+    def tokens_sent(buf):
+        for c in range(chunks):
+            tok_to_pair(buf, c).wait_send()
+            for i in range(1, groups):
+                tok_own(buf, c, i).wait_send()
+                tok_forward(buf, c, i).wait_send()
+
     @pl.when(is_first)
     def _():
-        for c in range(chunks):
-            tok_to_pair(c).wait_send()
-            for i in range(1, groups):
-                tok_own(c, i).wait_send()
-                tok_forward(c, i).wait_send()
+        tokens_sent(xs)
+        for i in range(1, groups):
+            to_peer(end, i).wait_send()
 
         @pl.loop(0, steps)
         def _(t):
-            for i in range(groups):
-                to_next(t, i).wait_send()
+            for g in range(groups):
+                to_next(t, g).wait_send()
 
         @pl.loop(0, keep)
         def _(t):
@@ -372,6 +447,10 @@
 
     @pl.when(is_last)
     def _():
+        tokens_sent(ts)
+        for c in range(chunks):
+            tok_over(c).wait_send()
+
         @pl.loop(0, keep)
         def _(t):
             top_far(t, 0).wait_send()
@@ -395,13 +474,16 @@
             jax.ShapeDtypeStruct((1, sentences, units), bf16),
             jax.ShapeDtypeStruct((1, sentences, units), f32),
         ),
-        in_specs=[vmem] * 4,
+        in_specs=[pl.BlockSpec(memory_space=pl.ANY)] * 3 + [vmem],
         out_specs=(vmem, vmem, vmem),
         scratch_shapes=[
             pltpu.VMEM((steps, groups, 2, half, units), bf16),
             pltpu.VMEM((steps, groups, 2, half, units), bf16),
+            pltpu.VMEM((steps // 2, groups, 2, half, units), bf16),
             pltpu.VMEM((2, depth, width), bf16),
             pltpu.VMEM((2, depth, width), bf16),
+            pltpu.VMEM((depth, width), bf16),
+            pltpu.VMEM((depth, width), bf16),
             pltpu.VMEM((depth, width), bf16),
             pltpu.VMEM((depth, width), bf16),
             pltpu.VMEM((1, width), f32),
@@ -411,8 +493,11 @@
             dma,
             dma((steps, groups)),
             dma((steps, groups)),
-            dma((steps // CHUNK,)),
-            dma((steps // CHUNK, groups, 2)),
+            dma((steps // CHUNK // 2,)),
+            dma((steps // CHUNK // 2, groups, 2)),
+            dma((steps // CHUNK // 2,)),
+            dma((steps // CHUNK // 2,)),
+            dma((2,)),
             dma((2,)),
             dma((2,)),
             dma,
@@ -439,7 +524,7 @@
     def body(tokens, w_input, w_recur, bias):
         steps, sentences, units = tokens.shape
         fits = mesh.shape["layer"] == 2 and mesh.shape["dp"] == 2 and cols % 2 == 0
-        fits = fits and units % 128 == 0 and sentences % 32 == 0 and steps % CHUNK == 0
+        fits = fits and units % 128 == 0 and sentences % 32 == 0 and steps % (2 * CHUNK) == 0
         return (fused if fits else shards)(tokens, w_input, w_recur, bias)
 
     return jax.shard_map(body, mesh=mesh, in_specs=in_specs, out_specs=out_specs, check_vma=False)

time: 169 us -> 127 us (0.75)
  Pallas kernels: 162 us -> 120 us
    pallas_call x1, Pallas kernels: 162 us -> 120 us  [fused(): pl.pallas_call(functools.partial(lstm_kernel, groups), out_shape=(jax.Sha...]
where the time goes in v2:
time: 127 us
  Pallas kernels  120 us (94%)
  local copies, waits for them, and re-layouts  6.11 us (5%)
    pallas_call x1, Pallas kernels, fused(): pl.pallas_call(functools.partial(lstm_kernel, groups), out_shape=(jax.Sha...  120 us
    unnamed x11, local copies, waits for them, and re-layouts  6.11 us

profile of v2, /device:TPU:6, one launch (start us, length us, event | category | flops | bytes accessed | tf_op | source)
XLA Modules:
  0.0 126.7 jit_solution(850323029740584130)
XLA Ops:
  0.6 0.0 copy-start.3
  0.6 0.7 copy-done.3
  1.3 0.0 copy-start
  1.3 1.2 copy-done
  2.5 0.0 copy-start.1
  2.5 1.2 copy-done.1
  3.8 0.0 copy-start.2
  3.8 1.0 copy-done.2
  4.8 119.9 %lstm.1 = (bf16[8,128,128]{2,1,0:T(8,128)(2,1)S(1)}, bf16[1,128,128]{2,1,0:T(8,128)(2,1)S(1)}, f32[1,128,128]{2,1,0:T(8,128)S(1)}) custom-call(bf16[16,128,128]{2,1,0:T(8,128)(2,1)S(1)} %copy-done.2, bf16[1024,512]{1,0:T(8,128)(2,1)S(1)} %bitcast.2, bf16[1024,512]{1,0:T(8,128)(2,1)S(1)} %bitcast.3, f32[1,512]{1,0:T(1,128)S(1)} %copy-done.3), custom_call_target="tpu_custom_call" | custom-call | tf_op jit(solution)/shard_map/lstm/pallas_call | solution.py:470
  124.8 0.7 copy.10
  125.5 0.6 copy.11
  126.1 0.6 copy.12
Async XLA Ops:
  0.6 0.7 copy-start.3
  1.3 1.2 copy-start
  2.5 1.2 copy-start.1
  3.8 1.0 copy-start.2

commit v3 on v2

--- a/solution.py
+++ b/solution.py
@@ -96,6 +96,7 @@
 
 MESH = pl.DeviceIdType.MESH
 CHUNK = 4
+SUBS = 2
 
 
 def lstm_kernel(
@@ -108,6 +109,7 @@
 ):
     steps, sentences, units = tokens.shape
     half = sentences // 2
+    sub = half // SUBS
     depth = w_in.shape[0]
     part_rows = depth // 2
     keep = steps // 2
@@ -132,6 +134,12 @@
     def near(i):
         return lax.rem(p + i, groups)
 
+    def nearest(i):
+        ranks = [sorted((abs(g - k), g) for g in range(groups))[i][1] for k in range(groups)]
+        return sum(jnp.where(p == k, g, 0) for k, g in enumerate(ranks))
+
+    peers = [nearest(i) for i in range(1, groups)]
+
     barrier = pltpu.get_barrier_semaphore()
     targets = [{"col": 2 * near(i) + q} for i in range(1, groups)]
     targets += [pair, twin]
@@ -304,31 +312,46 @@
             tok_all(ts, c)
             tok_over(c).start()
 
-    def to_peer(t, i):
-        return copy(hs.at[t, p], hs.at[t, p], h_sem.at[t, p], {"col": 2 * near(i) + q})
-
-    def from_peer(t, i):
-        return copy(hs.at[t, near(i)], hs.at[t, near(i)], h_sem.at[t, near(i)], pair)
-
-    def to_next(t, g):
-        return copy(hs.at[t, g], xs.at[t, g], x_sem.at[t, g], {"layer": 1 - level})
+    def to_peer(t, s, g):
+        return copy(hs.at[t, p, s], hs.at[t, p, s], h_sem.at[t, p, s], {"col": 2 * g + q})
+
+    def from_peer(t, s, g):
+        return copy(hs.at[t, g, s], hs.at[t, g, s], h_sem.at[t, g, s], pair)
+
+    def sub_rows(s):
+        return pl.ds(s * sub, sub)
+
+    def out_rows(y, s):
+        return pl.ds(pl.multiple_of(y * half + s * sub, sub), sub)
+
+    def to_next(t, s, g):
+        return copy(hs.at[t, g, s], xs.at[t, g, :, sub_rows(s)], x_sem.at[t, g, s], {"layer": 1 - level})
 
     def joined(ref, t):
         return jnp.concatenate([ref[t, g, y] for g in range(groups) for y in range(2)], axis=1)
 
-    def top_far(t, b):
-        return copy(hs.at[t, p, b], top.at[t, my_rows], top_sem.at[t, q], {"layer": 1 - level, "col": 2 * p + b})
-
-    def top_pair(t):
-        return copy(hs.at[t, p, other], top.at[t - keep, my_rows], top_sem.at[t - keep, q], pair)
-
-    def peers_in(t):
-        for i in range(1, groups):
-            from_peer(t, i).wait_recv()
-
-            @pl.when(is_first)
-            def _():
-                to_next(t, near(i)).start()
+    def top_far(t, s, b):
+        return copy(hs.at[t, p, s, b], top.at[t, out_rows(q, s)], top_sem.at[t, q, s], {"layer": 1 - level, "col": 2 * p + b})
+
+    def top_pair(t, s):
+        return copy(hs.at[t, p, s, other], top.at[t - keep, out_rows(q, s)], top_sem.at[t - keep, q, s], pair)
+
+    def top_in(t, y, s):
+        rows = top.at[t, out_rows(y, s)]
+        return copy(rows, rows, top_sem.at[t, y, s], pair)
+
+    def add_recurrent(t, s, g):
+        state = jnp.concatenate([hs[t, g, s, 0], hs[t, g, s, 1]], axis=1)
+        rows = pl.ds(pl.multiple_of(g * 2 * units, 2 * units), 2 * units)
+        for b in range(2):
+            gates[b, sub_rows(s)] += jnp.dot(state, wr[b, rows], preferred_element_type=jnp.float32)
+
+    def peer_in(t, s, g):
+        from_peer(t, s, g).wait_recv()
+
+        @pl.when(is_first)
+        def _():
+            to_next(t, s, g).start()
 
     @pl.loop(0, steps)
     def _(t):
@@ -348,7 +371,8 @@
         @pl.when(is_last)
         def _():
             for g in range(groups):
-                to_next(t, g).wait_recv()
+                for s in range(SUBS):
+                    to_next(t, s, g).wait_recv()
 
         given = joined(xs, t)
         for b in range(2):
@@ -363,63 +387,77 @@
 
         @pl.when(t > 0)
         def _():
-            peers_in(t - 1)
-            state = joined(hs, t - 1)
+            for s in range(SUBS):
+                add_recurrent(t - 1, s, p)
+
+        for s in range(SUBS):
+            rows = sub_rows(s)
+
+            @pl.when(t > 0)
+            def _():
+                for g in peers:
+                    peer_in(t - 1, s, g)
+                    add_recurrent(t - 1, s, g)
+
             for b in range(2):
-                gates[b] += jnp.dot(state, wr[b], preferred_element_type=jnp.float32)
-
-        for b in range(2):
-            in_gate = 0.5 * jnp.tanh(0.5 * gates[b, :, 0:units]) + 0.5
-            forget = 0.5 * jnp.tanh(0.5 * gates[b, :, units : 2 * units]) + 0.5
-            update = jnp.tanh(gates[b, :, 2 * units : 3 * units])
-            out_gate = 0.5 * jnp.tanh(0.5 * gates[b, :, 3 * units :]) + 0.5
-            cell_new = forget * cell[b] + in_gate * update
-            cell[b] = cell_new
-            hs[t, p, b] = (out_gate * jnp.tanh(cell_new)).astype(jnp.bfloat16)
-
-        @pl.when(is_first | (t < steps - 1))
-        def _():
-            for i in range(1, groups):
-                to_peer(t, i).start()
-
-        @pl.when(is_first)
-        def _():
-            to_next(t, p).start()
-
-        @pl.when(is_last & (t < keep))
-        def _():
-            top_far(t, 0).start()
-            top_far(t, 1).start()
-
-        @pl.when(is_last & (t >= keep))
-        def _():
-            top_pair(t).start()
-            top[t - keep, my_rows] = hs[t, p, q]
+                in_gate = 0.5 * jnp.tanh(0.5 * gates[b, rows, 0:units]) + 0.5
+                forget = 0.5 * jnp.tanh(0.5 * gates[b, rows, units : 2 * units]) + 0.5
+                update = jnp.tanh(gates[b, rows, 2 * units : 3 * units])
+                out_gate = 0.5 * jnp.tanh(0.5 * gates[b, rows, 3 * units :]) + 0.5
+                cell_new = forget * cell[b, rows] + in_gate * update
+                cell[b, rows] = cell_new
+                hs[t, p, s, b] = (out_gate * jnp.tanh(cell_new)).astype(jnp.bfloat16)
+
+            @pl.when(is_first | (t < steps - 1))
+            def _():
+                for g in reversed(peers):
+                    to_peer(t, s, g).start()
+
+            @pl.when(is_first)
+            def _():
+                to_next(t, s, p).start()
+
+            @pl.when(is_last & (t < keep))
+            def _():
+                top_far(t, s, 0).start()
+                top_far(t, s, 1).start()
+
+            @pl.when(is_last & (t >= keep))
+            def _():
+                top_pair(t, s).start()
+                top[t - keep, out_rows(q, s)] = hs[t, p, s, q]
 
     end = steps - 1
 
     @pl.when(is_first)
     def _():
-        peers_in(end)
-
-    fin_h = copy(hs.at[end, p, other], final_h.at[0, my_rows], fin_sem.at[0], pair)
-    fin_c = copy(cell.at[other], final_c.at[0, my_rows], fin_sem.at[1], pair)
-    fin_h.start()
+        for s in range(SUBS):
+            for g in peers:
+                peer_in(end, s, g)
+
+    def fin_h(s):
+        return copy(hs.at[end, p, s, other], final_h.at[0, out_rows(q, s)], fin_sem.at[1 + s], pair)
+
+    fin_c = copy(cell.at[other], final_c.at[0, my_rows], fin_sem.at[0], pair)
     fin_c.start()
-    final_h[0, my_rows] = hs[end, p, q]
     final_c[0, my_rows] = cell[q]
+    for s in range(SUBS):
+        fin_h(s).start()
+        final_h[0, out_rows(q, s)] = hs[end, p, s, q]
 
     bias_copy.wait_send()
     for k in range(2):
         w_to_pair(k).wait_send()
         w_to_twin(k).wait_send()
-    fin_h.wait()
     fin_c.wait()
+    for s in range(SUBS):
+        fin_h(s).wait()
 
     @pl.loop(0, end)
     def _(t):
-        for i in range(1, groups):
-            to_peer(t, i).wait_send()
+        for s in range(SUBS):
+            for g in peers:
+                to_peer(t, s, g).wait_send()
 
     def tokens_sent(buf):
         for c in range(chunks):
@@ -431,19 +469,21 @@
     @pl.when(is_first)
     def _():
         tokens_sent(xs)
-        for i in range(1, groups):
-            to_peer(end, i).wait_send()
+        for s in range(SUBS):
+            for g in peers:
+                to_peer(end, s, g).wait_send()
 
         @pl.loop(0, steps)
         def _(t):
-            for g in range(groups):
-                to_next(t, g).wait_send()
+            for s in range(SUBS):
+                for g in range(groups):
+                    to_next(t, s, g).wait_send()
 
         @pl.loop(0, keep)
         def _(t):
-            for y in range(2):
-                rows = top.at[t, pl.ds(y * half, half)]
-                copy(rows, rows, top_sem.at[t, y], pair).wait_recv()
+            for s in range(SUBS):
+                for y in range(2):
+                    top_in(t, y, s).wait_recv()
 
     @pl.when(is_last)
     def _():
@@ -453,11 +493,11 @@
 
         @pl.loop(0, keep)
         def _(t):
-            top_far(t, 0).wait_send()
-            top_far(t, 1).wait_send()
-            top_pair(t + keep).wait_send()
-            rows = top.at[t, other_rows]
-            copy(rows, rows, top_sem.at[t, other], pair).wait_recv()
+            for s in range(SUBS):
+                top_far(t, s, 0).wait_send()
+                top_far(t, s, 1).wait_send()
+                top_pair(t + keep, s).wait_send()
+                top_in(t, other, s).wait_recv()
 
 
 def fused(tokens, w_input, w_recur, bias):
@@ -474,11 +514,11 @@
             jax.ShapeDtypeStruct((1, sentences, units), bf16),
             jax.ShapeDtypeStruct((1, sentences, units), f32),
         ),
-        in_specs=[pl.BlockSpec(memory_space=pl.ANY)] * 3 + [vmem],
+        in_specs=[pl.BlockSpec(memory_space=pltpu.HBM)] * 3 + [vmem],
         out_specs=(vmem, vmem, vmem),
         scratch_shapes=[
             pltpu.VMEM((steps, groups, 2, half, units), bf16),
-            pltpu.VMEM((steps, groups, 2, half, units), bf16),
+            pltpu.VMEM((steps, groups, SUBS, 2, half // SUBS, units), bf16),
             pltpu.VMEM((steps // 2, groups, 2, half, units), bf16),
             pltpu.VMEM((2, depth, width), bf16),
             pltpu.VMEM((2, depth, width), bf16),
@@ -491,8 +531,8 @@
             pltpu.VMEM((2, half, units), f32),
             pltpu.VMEM((2, half, width), f32),
             dma,
-            dma((steps, groups)),
-            dma((steps, groups)),
+            dma((steps, groups, SUBS)),
+            dma((steps, groups, SUBS)),
             dma((steps // CHUNK // 2,)),
             dma((steps // CHUNK // 2, groups, 2)),
             dma((steps // CHUNK // 2,)),
@@ -501,11 +541,11 @@
             dma((2,)),
             dma((2,)),
             dma,
-            dma((steps // 2, 2)),
-            dma((2,)),
+            dma((steps // 2, 2, SUBS)),
+            dma((1 + SUBS,)),
         ],
         compiler_params=pltpu.CompilerParams(
-            collective_id=0, has_side_effects=True, vmem_limit_bytes=48 * 2**20
+            collective_id=0, has_side_effects=True, vmem_limit_bytes=67_000_000
         ),
         name="lstm",
     )(tokens, w_input[0], w_recur[0], bias)
@@ -524,7 +564,7 @@
     def body(tokens, w_input, w_recur, bias):
         steps, sentences, units = tokens.shape
         fits = mesh.shape["layer"] == 2 and mesh.shape["dp"] == 2 and cols % 2 == 0
-        fits = fits and units % 128 == 0 and sentences % 32 == 0 and steps % (2 * CHUNK) == 0
+        fits = fits and units % 128 == 0 and sentences % (32 * SUBS) == 0 and steps % (2 * CHUNK) == 0
         return (fused if fits else shards)(tokens, w_input, w_recur, bias)
 
     return jax.shard_map(body, mesh=mesh, in_specs=in_specs, out_specs=out_specs, check_vma=False)

time: 127 us -> 114 us (0.90)
  Pallas kernels: 120 us -> 110 us
  local copies, waits for them, and re-layouts: 6.11 us -> 3.16 us
    pallas_call x1, Pallas kernels: 120 us -> 110 us  [fused(): pl.pallas_call(functools.partial(lstm_kernel, groups), out_shape=(jax.Sha...]
    unnamed x11 -> x7, local copies, waits for them, and re-layouts: 6.11 us -> 3.16 us
where the time goes in v3:
time: 114 us
  Pallas kernels  110 us (96%)
  local copies, waits for them, and re-layouts  3.16 us (3%)
    pallas_call x1, Pallas kernels, fused(): pl.pallas_call(functools.partial(lstm_kernel, groups), out_shape=(jax.Sha...  110 us
    unnamed x7, local copies, waits for them, and re-layouts  3.16 us

profile of v3, /device:TPU:6, one launch (start us, length us, event | category | flops | bytes accessed | tf_op | source)
XLA Modules:
  0.0 114.1 jit_solution(10849350029640140626)
XLA Ops:
  0.6 110.3 %lstm.1 = (bf16[8,128,128]{2,1,0:T(8,128)(2,1)}, bf16[1,128,128]{2,1,0:T(8,128)(2,1)}, f32[1,128,128]{2,1,0:T(8,128)}) custom-call(bf16[16,128,128]{2,1,0:T(8,128)(2,1)} %tokens.1, bf16[1024,512]{1,0:T(8,128)(2,1)} %bitcast.2, bf16[1024,512]{1,0:T(8,128)(2,1)} %bitcast.3, f32[1,512]{1,0:T(1,128)} %bias.1), custom_call_target="tpu_custom_call" | custom-call | tf_op jit(solution)/shard_map/lstm/pallas_call | solution.py:510
  110.9 0.0 copy-start.1
  110.9 1.7 %copy.10 = bf16[8,128,128]{2,1,0:T(8,128)(2,1)} copy(bf16[8,128,128]{2,1,0:T(8,128)(2,1)} %get-tuple-element.6) | data formatting | bytes 524288
  112.6 0.0 copy-done.1
  112.6 0.0 copy-start
  112.6 0.6 copy.11
  113.2 0.2 copy-done
  113.4 0.6 copy.12
Async XLA Ops:
  110.9 1.7 %copy-start.1 = (bf16[1,128,128]{2,1,0:T(8,128)(2,1)S(1)}, bf16[1,128,128]{2,1,0:T(8,128)(2,1)}, u32[]{:S(2)}) copy-start(bf16[1,128,128]{2,1,0:T(8,128)(2,1)} %get-tuple-element.7) | copy-start | bytes 98308
  112.6 0.9 copy-start

commit v4 on v3

--- a/solution.py
+++ b/solution.py
@@ -97,6 +97,7 @@
 MESH = pl.DeviceIdType.MESH
 CHUNK = 4
 SUBS = 2
+PIECES = 2
 
 
 def lstm_kernel(
@@ -186,21 +187,23 @@
             tok_arrived(buf, c, i, 0).wait_recv()
             tok_arrived(buf, c, i, 1).wait_recv()
 
-    part = pl.ds(pl.multiple_of(dp * part_rows, part_rows), part_rows)
-    twin_part = pl.ds(pl.multiple_of((1 - dp) * part_rows, part_rows), part_rows)
     weights = ((w_in, raw_in), (w_rec, raw_rec))
-
-    def w_to_pair(k):
+    piece_rows = part_rows // PIECES
+
+    def piece(core, n):
+        return pl.ds(pl.multiple_of(core * part_rows + n * piece_rows, piece_rows), piece_rows)
+
+    def w_to_pair(k, n):
         own, raw = weights[k]
-        return copy(own.at[part], raw.at[part], w_y_sem.at[k], pair)
-
-    def w_to_twin(k):
+        return copy(own.at[piece(dp, n)], raw.at[piece(dp, n)], w_y_sem.at[k, n], pair)
+
+    def w_to_twin(k, n):
         raw = weights[k][1]
-        return copy(raw.at[part], raw.at[part], w_d_sem.at[k], twin)
-
-    def w_from_twin(k):
+        return copy(raw.at[piece(dp, n)], raw.at[piece(dp, n)], w_d_sem.at[k, n], twin)
+
+    def w_from_twin(k, n):
         raw = weights[k][1]
-        return copy(raw.at[twin_part], raw.at[twin_part], w_d_sem.at[k], twin)
+        return copy(raw.at[piece(1 - dp, n)], raw.at[piece(1 - dp, n)], w_d_sem.at[k, n], twin)
 
     bias_copy = copy(bias, braw, b_sem, pair)
 
@@ -222,7 +225,8 @@
 
     own_weights(0).start()
     bias_copy.start()
-    w_to_pair(0).start()
+    for n in range(PIECES):
+        w_to_pair(0, n).start()
 
     @pl.when(is_first)
     def _():
@@ -237,7 +241,6 @@
             tok_local(ts, c).start()
 
     own_weights(1).start()
-    w_to_pair(1).start()
 
     cell[...] = jnp.zeros_like(cell)
     width = 4 * units
@@ -253,6 +256,22 @@
             rows = pl.ds(pl.multiple_of(r * block_rows, block_rows), block_rows)
             moved = jnp.dot(src[rows], order, preferred_element_type=jnp.float32)
             dst[which, rows] = moved.astype(jnp.bfloat16)
+
+    def regroup_piece(src, dst, rows):
+        moved = jnp.dot(src[rows], order, preferred_element_type=jnp.float32)
+        dst[other, rows] = moved.astype(jnp.bfloat16)
+
+    def swap_weights(k, dst):
+        raw = weights[k][1]
+        for n in range(PIECES):
+            w_to_pair(k, n).wait_recv()
+            w_to_twin(k, n).start()
+            if k == 0:
+                w_to_pair(1, n).start()
+            regroup_piece(raw, dst, piece(dp, n))
+        for n in range(PIECES):
+            w_from_twin(k, n).wait_recv()
+            regroup_piece(raw, dst, piece(1 - dp, n))
 
     def regroup_bias(src, which):
         value = jnp.broadcast_to(src[...], (8, width))
@@ -293,10 +312,7 @@
     regroup(own_rec, wr, q)
     bias_copy.wait_recv()
     regroup_bias(braw, other)
-    w_to_pair(0).wait_recv()
-    w_to_twin(0).start()
-    w_from_twin(0).wait_recv()
-    regroup(raw_in, wi, other)
+    swap_weights(0, wi)
 
     @pl.when(is_first)
     def _():
@@ -380,10 +396,7 @@
 
         @pl.when(t == 1)
         def _():
-            w_to_pair(1).wait_recv()
-            w_to_twin(1).start()
-            w_from_twin(1).wait_recv()
-            regroup(raw_rec, wr, other)
+            swap_weights(1, wr)
 
         @pl.when(t > 0)
         def _():
@@ -447,8 +460,9 @@
 
     bias_copy.wait_send()
     for k in range(2):
-        w_to_pair(k).wait_send()
-        w_to_twin(k).wait_send()
+        for n in range(PIECES):
+            w_to_pair(k, n).wait_send()
+            w_to_twin(k, n).wait_send()
     fin_c.wait()
     for s in range(SUBS):
         fin_h(s).wait()
@@ -538,14 +552,14 @@
             dma((steps // CHUNK // 2,)),
             dma((steps // CHUNK // 2,)),
             dma((2,)),
-            dma((2,)),
-            dma((2,)),
+            dma((2, PIECES)),
+            dma((2, PIECES)),
             dma,
             dma((steps // 2, 2, SUBS)),
             dma((1 + SUBS,)),
         ],
         compiler_params=pltpu.CompilerParams(
-            collective_id=0, has_side_effects=True, vmem_limit_bytes=67_000_000
+            collective_id=0, has_side_effects=True, vmem_limit_bytes=66_590_000
         ),
         name="lstm",
     )(tokens, w_input[0], w_recur[0], bias)

time: 114 us -> 114 us (level); the launches traced: 114 us -> 112 us
    pallas_call x1, Pallas kernels: 110 us -> 109 us  [fused(): pl.pallas_call(functools.partial(lstm_kernel, groups), out_shape=(jax.Sha...]
where the time goes in v4:
time: 114 us; the launch traced here: 112 us
  Pallas kernels  109 us (96%)
  local copies, waits for them, and re-layouts  3.16 us (3%)
    pallas_call x1, Pallas kernels, fused(): pl.pallas_call(functools.partial(lstm_kernel, groups), out_shape=(jax.Sha...  109 us
    unnamed x7, local copies, waits for them, and re-layouts  3.16 us

profile of v4, /device:TPU:6, one launch (start us, length us, event | category | flops | bytes accessed | tf_op | source)
XLA Modules:
  0.0 112.4 jit_solution(12903485435637122749)
XLA Ops:
  0.6 108.6 %lstm.1 = (bf16[8,128,128]{2,1,0:T(8,128)(2,1)}, bf16[1,128,128]{2,1,0:T(8,128)(2,1)}, f32[1,128,128]{2,1,0:T(8,128)}) custom-call(bf16[16,128,128]{2,1,0:T(8,128)(2,1)} %tokens.1, bf16[1024,512]{1,0:T(8,128)(2,1)} %bitcast.2, bf16[1024,512]{1,0:T(8,128)(2,1)} %bitcast.3, f32[1,512]{1,0:T(1,128)} %bias.1), custom_call_target="tpu_custom_call" | custom-call | tf_op jit(solution)/shard_map/lstm/pallas_call | solution.py:524
  109.3 0.0 copy-start.1
  109.3 1.7 %copy.10 = bf16[8,128,128]{2,1,0:T(8,128)(2,1)} copy(bf16[8,128,128]{2,1,0:T(8,128)(2,1)} %get-tuple-element.6) | data formatting | bytes 524288
  110.9 0.0 copy-done.1
  110.9 0.0 copy-start
  110.9 0.6 copy.11
  111.6 0.2 copy-done
  111.8 0.6 copy.12
Async XLA Ops:
  109.3 1.7 %copy-start.1 = (bf16[1,128,128]{2,1,0:T(8,128)(2,1)S(1)}, bf16[1,128,128]{2,1,0:T(8,128)(2,1)}, u32[]{:S(2)}) copy-start(bf16[1,128,128]{2,1,0:T(8,128)(2,1)} %get-tuple-element.7) | copy-start | bytes 98308
  110.9 0.9 copy-start
